TPU v7x, 512 devices: a whole 4x4x16 slice. The times are simulated.
512 devices in a mesh: batch: 8 (over x, y_lo), seq: 32 (over y_hi, z), section: 2 (over core).
Axes of the slice: x: 4, y: 4 (y_hi: 2, y_lo: 2; y = y_hi * 2 + y_lo), z: 16, core: 2. Of those that a mesh axis runs over, the one named last changes fastest.
Arguments:
- acts: bfloat16 [2, 118784, 5120], P('section', ('batch', 'seq')), may hold values from -13 to 13
- cotangent: float32 [2, 118784, 6], P('section', ('batch', 'seq')), may hold values from -120 to 120
- routes: int32 [2, 118784, 6], P('section', ('batch', 'seq')), may hold values from 0 to 159, all different within a row
- router_weight: bfloat16 [2, 5120, 160], P('section', ('batch', 'seq')), may hold values from -0.078125 to 0.078125
Outputs:
- grad_router: float32 [2, 5120, 160], P('section', ('batch', 'seq'))
Inputs may be any that keep to these rules, and one draw needn't show every extreme that they name: `routes`: each token's row names 6 different experts, and every expert is named by some token.
All inputs are finite; a program needn't handle non-finite values.
Results may differ from a plain program's by a relative error of at most 0.0017.
Values may be sent and summed in bfloat16 or wider, within the bound.
No kernel may reach another device: no remote copies, remote signals or barrier semaphores. Data moves between devices by JAX's collectives and lax.ppermute only.
A program may use at most 64 MiB of HBM per device.

v0:
```python
import functools
import math

import jax
import jax.numpy as jnp
from jax import lax
from jax.sharding import Mesh
from jax.sharding import PartitionSpec as P

BATCH_SEQ = ("batch_0", "batch_1", "seq_0", "seq_1")
SEQ = ("seq_0", "seq_1")
BATCH = ("batch_0", "batch_1")
BATCH_SEQ_SECTION = ("batch_0", "batch_1", "seq_0", "seq_1", "section")


def laid_out(parts, dim):
    parts = jnp.moveaxis(parts, 0, dim)
    shape = parts.shape
    return parts.reshape(*shape[:dim], shape[dim] * shape[dim + 1], *shape[dim + 2 :])


def stacked_from(x, axes, order):
    parts = x
    for k in order:
        parts = lax.all_gather(parts, axes[k])
    done = order[::-1]
    back = [done.index(k) for k in range(len(axes))]
    parts = parts.transpose(*back, *range(len(axes), parts.ndim))
    return parts.reshape(-1, *x.shape)


def gather_axes(x, axes, order, dim):
    return laid_out(stacked_from(x, axes, order), dim)


def split_up(x, dim, peers):
    before, after = (x.shape[:dim], x.shape[dim + 1 :])
    return jnp.moveaxis(x.reshape(*before, peers, -1, *after), dim, 0)


def summed_on_arrival(x, axis, dim):
    parts = split_up(x, dim, lax.axis_size(axis))
    arrived = lax.all_to_all(parts, axis, split_axis=0, concat_axis=0, tiled=True)
    return arrived.sum(axis=0)


def over_axes_2(x, axes):
    return functools.reduce(lax.psum, axes, x)


def shards(acts, cotangent, routes, router_weight):
    layers = acts.shape[0]
    width = acts.shape[2]
    experts = router_weight.shape[2]
    x_part = acts
    logits = jnp.einsum(
        "ltd,lde->lte",
        x_part,
        gather_axes(router_weight, BATCH_SEQ, (2, 1, 0, 3), 1),
        preferred_element_type=jnp.float32,
    )
    expo = jnp.exp(logits)
    probs = expo / jnp.sum(expo, axis=-1, keepdims=True)
    expert_ids = jnp.arange(experts, dtype=jnp.int32)
    picks = (routes[:, :, :, None] == expert_ids[None, None, None, :]).astype(jnp.float32)
    d_prob = jnp.sum(cotangent[:, :, :, None] * picks, axis=2)
    inner = jnp.sum(probs * d_prob, axis=-1, keepdims=True)
    d_logits = (probs * (d_prob - inner)).astype(jnp.bfloat16)
    x_part = acts
    batch_rows = summed_on_arrival(
        jnp.einsum("ltd,lte->dle", x_part, d_logits, preferred_element_type=jnp.float32), BATCH, 0
    )
    summed = summed_on_arrival(batch_rows, SEQ, 0)
    summed = jnp.transpose(summed, (1, 0, 2))
    local_squares = jnp.sum(summed * summed)
    square_sum = over_axes_2(local_squares, BATCH_SEQ_SECTION)
    entry_count = 1.0 * layers * lax.axis_size("section") * width * experts
    clip_norm = 0.25 * math.sqrt(entry_count)
    clip_scale = jnp.minimum(jnp.float32(1.0), clip_norm / jnp.sqrt(square_sum))
    return summed * clip_scale


def solution(mesh):
    torus = Mesh(
        mesh.devices.reshape(4, 2, 2, 16, mesh.shape["section"]),
        ("batch_0", "batch_1", "seq_0", "seq_1", "section"),
    )
    placed = (
        P("section", BATCH_SEQ, None),
        P("section", BATCH_SEQ, None),
        P("section", BATCH_SEQ, None),
        P("section", BATCH_SEQ, None),
    )
    return jax.shard_map(
        shards,
        mesh=torus,
        in_specs=placed,
        out_specs=P("section", BATCH_SEQ, None),
        check_vma=False,
    )
```

profile of v0, /device:TPU:1, one launch (start us, length us, event | category | flops | bytes accessed | tf_op | source)
XLA Modules:
  0.0 260.9 jit_solution(16855208796825774544)
XLA Ops:
  6.5 5.8 %all-gather = bf16[2,20,160]{2,1,0:T(8,128)(2,1)S(1)} all-gather(bf16[1,20,160]{2,1,0:T(8,128)(2,1)} %param.7), channel_id=2, replica_groups=mesh['batch_0'=4,'batch_1'=2,'seq_0'=2,'seq_1'=16,'section'=2] {'seq_0'}, dimensions={0}, use_global_device_ids=true | all-gather | bytes 19200 | tf_op jit(solution)/shard_map/all_gather | solution.py:25
  12.3 3.3 %all-gather.1 = bf16[4,20,160]{2,1,0:T(8,128)(2,1)S(1)} all-gather(bf16[2,20,160]{2,1,0:T(8,128)(2,1)S(1)} %all-gather), channel_id=3, replica_groups=mesh['batch_0'=4,'batch_1'=2,'seq_0'=2,'seq_1'=16,'section'=2] {'batch_1'}, dimensions={0}, use_global_device_ids=true | all-gather | bytes 38400 | tf_op jit(solution)/shard_map/all_gather | solution.py:25
  15.7 10.3 %all-gather.2 = bf16[8,2,1,20,160]{4,1,3,2,0:T(2,128)(2,1)} all-gather(bf16[2,2,1,20,160]{4,1,3,2,0:T(2,128)(2,1)S(1)} %copy.22), channel_id=4, replica_groups=mesh['batch_0'=4,'batch_1'=2,'seq_0'=2,'seq_1'=16,'section'=2] {'batch_0'}, dimensions={0}, use_global_device_ids=true | all-gather | bytes 128000 | tf_op jit(solution)/shard_map/all_gather | solution.py:25
  26.0 0.7 copy.37
  26.7 0.7 copy.38
  27.4 0.3 select_reduce_fusion
  27.7 72.2 %all-gather.6.cloned.1.call-done = bf16[64,2,2,1,20,160]{5,2,4,3,1,0:T(2,128)(2,1)} async-done(((bf16[4,2,2,1,20,160]{5,2,4,3,1,0:T(2,128)(2,1)}), bf16[64,2,2,1,20,160]{5,2,4,3,1,0:T(2,128)(2,1)}) %all-gather.6.cloned.1.call-update) | async-done | bytes 1638416 | tf_op jit(solution)/shard_map/all_gather | solution.py:25
  99.8 3.9 %copy.24 = bf16[4,2,2,16,1,20,160]{6,5,3,2,1,0,4:T(8,128)(2,1)} copy(bf16[4,2,2,16,1,20,160]{6,2,5,1,0,3,4:T(2,128)(2,1)} %bitcast.36) | data formatting | bytes 3276800 | tf_op jit(solution)/shard_map/transpose | solution.py:28
  103.7 4.1 %reshape.79 = bf16[5120,160]{1,0:T(8,128)(2,1)S(1)} reshape(bf16[4,2,2,16,1,20,160]{6,5,3,2,1,0,4:T(8,128)(2,1)} %copy.24) | data formatting | bytes 3276800 | tf_op jit(solution)/shard_map/reshape.1
  107.9 4.0 %fusion.8 = (f32[464]{0:T(512)S(1)}, f32[464,160]{0,1:T(8,128)S(1)}) fusion(bf16[5120,160]{1,0:T(8,128)(2,1)S(1)} %reshape.79, bf16[1,464,5120]{2,1,0:T(8,128)(2,1)} %param.4), kind=kOutput, calls=%fused_computation.16 | convolution fusion | flops 760291392 | bytes 6688576 | tf_op jit(solution)/shard_map/ltd,lde->lte/dot_general | solution.py:56
  112.0 1.0 fusion
  113.3 33.6 %all_to_all.10 = f32[8,640,1,160]{1,3,2,0:T(8,128)S(1)} all-to-all(f32[8,640,1,160]{1,3,2,0:T(8,128)S(1)} %bitcast.35), channel_id=1, replica_groups=mesh['batch_0'=4,'batch_1'=2,'seq_0'=2,'seq_1'=16,'section'=2] {'batch_0..., dimensions={0} | all-to-all | bytes 6553600 | tf_op jit(solution)/shard_map/all_to_all | solution.py:43
  146.9 0.9 reduce_sum.57
  147.8 1.2 copy.27
  149.0 0.8 reshape.86
  149.8 33.0 %all_to_all.11 = f32[32,20,1,160]{3,2,1,0:T(1,128)S(1)} all-to-all(f32[32,20,1,160]{3,2,1,0:T(1,128)S(1)} %reshape.86), channel_id=1, replica_groups=mesh['batch_0'=4,'batch_1'=2,'seq_0'=2,'seq_1'=16,'section'=2] {'seq_0',..., dimensions={0} | all-to-all | bytes 819200 | tf_op jit(solution)/shard_map/all_to_all | solution.py:43
  182.8 0.5 reduce_sum.58
  183.3 0.6 multiply_reduce_fusion.1
  183.9 8.0 %psum.35 = f32[]{:T(128)} all-reduce(f32[]{:T(128)} %multiply_reduce_fusion.1), channel_id=1, replica_groups=mesh['batch_0'=4,'batch_1'=2,'seq_0'=2,'seq_1'=16,'section'=2] {'batch_0'}, use_global_device_ids=true, to_apply=%region_6.0 | all-reduce | flops 1 | bytes 8 | tf_op jit(solution)/shard_map/psum | solution.py:48
  191.9 4.7 %psum.36 = f32[]{:T(128)} all-reduce(f32[]{:T(128)} %psum.35), channel_id=1, replica_groups=mesh['batch_0'=4,'batch_1'=2,'seq_0'=2,'seq_1'=16,'section'=2] {'batch_1'}, use_global_device_ids=true, to_apply=%region_7.0 | all-reduce | flops 1 | bytes 8 | tf_op jit(solution)/shard_map/psum | solution.py:48
  196.6 5.9 %psum.37 = f32[]{:T(128)} all-reduce(f32[]{:T(128)} %psum.36), channel_id=1, replica_groups=mesh['batch_0'=4,'batch_1'=2,'seq_0'=2,'seq_1'=16,'section'=2] {'seq_0'}, use_global_device_ids=true, to_apply=%region_8.0 | all-reduce | flops 1 | bytes 8 | tf_op jit(solution)/shard_map/psum | solution.py:48
  202.5 23.5 %psum.38 = f32[]{:T(128)} all-reduce(f32[]{:T(128)} %psum.37), channel_id=1, replica_groups=mesh['batch_0'=4,'batch_1'=2,'seq_0'=2,'seq_1'=16,'section'=2] {'seq_1'}, use_global_device_ids=true, to_apply=%region_9.0 | all-reduce | flops 1 | bytes 8 | tf_op jit(solution)/shard_map/psum | solution.py:48
  226.0 26.8 %psum.39 = f32[]{:T(128)} all-reduce(f32[]{:T(128)} %psum.38), channel_id=1, replica_groups=mesh['batch_0'=4,'batch_1'=2,'seq_0'=2,'seq_1'=16,'section'=2] {'section'}, use_global_device_ids=true, to_apply=%region_10.0 | all-reduce | flops 1 | bytes 8 | tf_op jit(solution)/shard_map/psum | solution.py:48
  253.5 0.6 mul.51
  (11 shorter events, 0.4 us)
Async XLA Ops:
  6.5 93.3 %all-gather.6.cloned.1.call-start = ((), (), s32[]{:S(2)}) async-start(), calls=%async_computation.2 | async-start | bytes 2785280 | tf_op jit(solution)/shard_map/all_gather | solution.py:25
  103.7 8.3 %slice-start = ((s8[4751360]{0:T(1024)(128)(4,1)}), s8[557056]{0:T(1024)(128)(4,1)S(1)}, s32[]{:S(2)}) async-start(s8[4751360]{0:T(1024)(128)(4,1)} %bitcast.32), calls=%async_computation.3 | async-start | bytes 1114112
  107.9 4.1 %slice-start.1 = ((s8[4751360]{0:T(1024)(128)(4,1)}), s8[4194304]{0:T(1024)(128)(4,1)S(1)}, s32[]{:S(2)}) async-start(s8[4751360]{0:T(1024)(128)(4,1)} %bitcast.32), calls=%async_computation.4 | async-start | bytes 8388608
Sparse Core Ops, SparseCore 0:
  26.1 73.6 all-gather.5
where the time goes:
time: 261 us
  blocking collectives  155 us (59%)
  waiting for transfers between devices  72.2 us (28%)
  between operations  14.2 us (5%)
  local copies, waits for them, and re-layouts  12.4 us (5%)
  matrix products  5.07 us (2%)
    all_gather x1, waiting for transfers between devices, stacked_from(): parts = lax.all_gather(parts, axes[k])  72.2 us
    psum x5, blocking collectives, over_axes_2(): return functools.reduce(lax.psum, axes, x)  68.9 us
    all_to_all x2, blocking collectives, summed_on_arrival(): lax.all_to_all(parts, axis, split_axis=0, concat_axis=0, tiled=True)  66.5 us
    all_gather x3, blocking collectives, stacked_from(): parts = lax.all_gather(parts, axes[k])  19.4 us
  transfers between devices with their start and end apart: 1, of which 1 were waited for; matrix products, arithmetic and copies ran while one was open for 1% of the time, Pallas kernels for 0%

commit v1 on v0

v1 whole, which is shorter than its diff:
```python
import math

import jax
import jax.numpy as jnp
from jax import lax
from jax.sharding import Mesh
from jax.sharding import PartitionSpec as P

BATCH_SEQ = ("batch_0", "batch_1", "seq_0", "seq_1")
PLANE = ("batch_0", "batch_1", "seq_0")
LINE = ("seq_1",)


def exchanged(parts, axes):
    return lax.all_to_all(parts, axes, split_axis=0, concat_axis=0, tiled=True)


def size(axes):
    return math.prod(lax.axis_size(a) for a in axes)


def gathered(x, axes):
    return exchanged(jnp.broadcast_to(x[None], (size(axes), *x.shape)), axes)


def shards(acts, cotangent, routes, router_weight):
    x = acts[0]
    width = x.shape[1]
    rows, experts = router_weight.shape[1:]
    plane, line = size(PLANE), size(LINE)
    weight = gathered(router_weight.reshape(1, rows * experts), LINE)
    weight = gathered(weight.reshape(-1, 128), PLANE)
    weight = weight.reshape(width, experts)
    logits = jnp.dot(x, weight, preferred_element_type=jnp.float32)
    expo = jnp.exp(logits)
    probs = expo / jnp.sum(expo, axis=-1, keepdims=True)
    expert_ids = jnp.arange(experts, dtype=jnp.int32)
    picks = (routes[0][:, :, None] == expert_ids[None, None, :]).astype(jnp.float32)
    d_prob = jnp.sum(cotangent[0][:, :, None] * picks, axis=1)
    inner = jnp.sum(probs * d_prob, axis=-1, keepdims=True)
    d_logits = (probs * (d_prob - inner)).astype(jnp.bfloat16)
    raw = jnp.einsum("td,te->de", x, d_logits, preferred_element_type=jnp.float32)
    parts = raw.astype(jnp.bfloat16).reshape(plane, -1, 128)
    summed = exchanged(parts, PLANE).astype(jnp.float32).sum(axis=0)
    parts = summed.reshape(line, 1, -1)
    summed = exchanged(parts, LINE).sum(axis=0).reshape(rows, experts)
    squares = jnp.sum(summed * summed)
    for axes in (PLANE, LINE):
        squares = jnp.sum(gathered(jnp.broadcast_to(squares, (1, 128)), axes)[:, 0, 0])
    squares = lax.psum(squares, "section")
    entry_count = 1.0 * lax.axis_size("section") * width * experts
    clip_norm = 0.25 * math.sqrt(entry_count)
    clip_scale = jnp.minimum(jnp.float32(1.0), clip_norm / jnp.sqrt(squares))
    return (summed * clip_scale)[None]


def solution(mesh):
    torus = Mesh(
        mesh.devices.reshape(4, 2, 2, 16, mesh.shape["section"]),
        ("batch_0", "batch_1", "seq_0", "seq_1", "section"),
    )
    placed = P("section", BATCH_SEQ, None)
    return jax.shard_map(
        shards,
        mesh=torus,
        in_specs=(placed, placed, placed, placed),
        out_specs=placed,
        check_vma=False,
    )
```

time: 261 us -> 173 us (0.66)
  waiting for transfers between devices: 72.2 us -> 20 us
  blocking collectives: 155 us -> 114 us
  between operations: 14.2 us -> 0.83 us
  starting transfers between devices: 0.01 us -> 6.8 us
  local copies, waits for them, and re-layouts: 12.4 us -> 17.4 us
  matrix products: 5.07 us -> 8.46 us
    all_gather x1 -> x0, waiting for transfers between devices: 72.2 us -> none  [stacked_from(): parts = lax.all_gather(parts, axes[k])]
    psum x5 -> x1, blocking collectives: 68.9 us -> 6.26 us  [shards(): squares = lax.psum(squares, 'section')]
    all_to_all x2 -> x5, blocking collectives: 66.5 us -> 108 us  [exchanged(): return lax.all_to_all(parts, axes, split_axis=0, concat_axis=0, tiled=True)]
    all_to_all x0 -> x1, waiting for transfers between devices: none -> 20 us  [exchanged(): return lax.all_to_all(parts, axes, split_axis=0, concat_axis=0, tiled=True)]
    all_gather x3 -> x0, blocking collectives: 19.4 us -> none  [stacked_from(): parts = lax.all_gather(parts, axes[k])]
    reshape x2, local copies, waits for them, and re-layouts: 1.02 us -> 9.13 us  [the longest x1 5.13 us: shards(): parts = raw.astype(jnp.bfloat16).reshape(plane, -1, 128)]
    all_to_all x0 -> x1, starting transfers between devices: none -> 6.8 us  [exchanged(): return lax.all_to_all(parts, axes, split_axis=0, concat_axis=0, tiled=True)]
    transpose x1 -> x0, local copies, waits for them, and re-layouts: 3.93 us -> none  [stacked_from(): parts = parts.transpose(*back, *range(len(axes), parts.ndim))]
  transfers between devices with their start and end apart: 1 -> 1, of which waited for: 1 -> 1; matrix products, arithmetic and copies ran while one was open for 1% -> 0% of each run, Pallas kernels for 0% -> 0%
where the time goes in v1:
time: 173 us; the launch traced here: 172 us
  blocking collectives  114 us (66%)
  waiting for transfers between devices  20 us (12%)
  local copies, waits for them, and re-layouts  17.4 us (10%)
  matrix products  8.46 us (5%)
  starting transfers between devices  6.8 us (4%)
  other arithmetic  4.36 us (3%)
    all_to_all x5, blocking collectives, exchanged(): return lax.all_to_all(parts, axes, split_axis=0, concat_axis=0, tiled=True)  108 us
    all_to_all x1, waiting for transfers between devices, exchanged(): return lax.all_to_all(parts, axes, split_axis=0, concat_axis=0, tiled=True)  20 us
    all_to_all x1, starting transfers between devices, exchanged(): return lax.all_to_all(parts, axes, split_axis=0, concat_axis=0, tiled=True)  6.8 us
    psum x1, blocking collectives, shards(): squares = lax.psum(squares, 'section')  6.26 us
    reshape x1, local copies, waits for them, and re-layouts, shards(): parts = raw.astype(jnp.bfloat16).reshape(plane, -1, 128)  5.13 us
    dot_general x1, matrix products, shards(): jnp.einsum('td,te->de', x, d_logits, preferred_element_type=jnp.float32)  4.56 us
    reshape x1, local copies, waits for them, and re-layouts, shards(): weight = weight.reshape(width, experts)  4 us
    dot_general x1, matrix products, shards(): logits = jnp.dot(x, weight, preferred_element_type=jnp.float32)  3.89 us
  transfers between devices with their start and end apart: 1, of which 1 were waited for; matrix products, arithmetic and copies ran while one was open for 0% of the time, Pallas kernels for 0%

profile of v1, /device:TPU:1, one launch (start us, length us, event | category | flops | bytes accessed | tf_op | source)
XLA Modules:
  0.0 172.3 jit_solution(7754784688436780291)
XLA Ops:
  0.0 0.8 broadcast_in_dim.8
  0.9 0.5 broadcast.18
  1.4 1.2 reduce.6
  2.8 27.5 %all_to_all.30 = bf16[16,2,1600]{2,1,0:T(2,128)(2,1)S(1)} all-to-all(bf16[16,2,1600]{2,1,0:T(2,128)(2,1)S(1)} %reshape.38), channel_id=1, replica_groups=mesh['batch_0'=4,'batch_1'=2,'seq_0'=2,'seq_1'=16,'section'=2] {'seq_1'}, dimensions={0} | all-to-all | bytes 204800 | tf_op jit(solution)/shard_map/all_to_all | solution.py:15
  30.5 0.6 reduce.5
  31.2 1.4 broadcast_in_dim.21
  32.6 6.8 %all-to-all-start.1 = ((bf16[16,400,128]{2,1,0:T(8,128)(2,1)}), bf16[16,400,128]{2,1,0:T(8,128)(2,1)}, u32[]{:S(2)}, u32[]{:S(2)}) async-start(bf16[16,400,128]{2,1,0:T(8,128)(2,1)} %broadcast_in_dim.21), calls=%async_computation.1 | async-start | bytes 3276800 | tf_op jit(solution)/shard_map/all_to_all | solution.py:15
  39.7 20.0 %all-to-all-done.1 = bf16[16,400,128]{2,1,0:T(8,128)(2,1)} async-done(((bf16[16,400,128]{2,1,0:T(8,128)(2,1)}), bf16[16,400,128]{2,1,0:T(8,128)(2,1)}, u32[]{:S(2)}, u32[]{:S(2)}) %all-to-all-start.1) | async-done | bytes 1638432 | tf_op jit(solution)/shard_map/all_to_all | solution.py:15
  59.7 4.0 %reshape.34 = bf16[5120,160]{1,0:T(8,128)(2,1)S(1)} reshape(bf16[16,400,128]{2,1,0:T(8,128)(2,1)} %all-to-all-done.1) | data formatting | bytes 3276800 | tf_op jit(solution)/shard_map/reshape | solution.py:33
  63.7 3.9 %fusion.8 = (f32[464]{0:T(512)S(1)}, f32[464,160]{0,1:T(8,128)S(1)}) fusion(bf16[5120,160]{1,0:T(8,128)(2,1)S(1)} %reshape.34, bf16[1,464,5120]{2,1,0:T(8,128)(2,1)} %param.4), kind=kOutput, calls=%fused_computation.19 | convolution fusion | flops 760291392 | bytes 6688576 | tf_op jit(solution)/shard_map/dot_general | solution.py:34
  67.7 4.6 %fusion = bf16[5120,160]{0,1:T(8,128)(2,1)} fusion(bf16[1,464,5120]{2,1,0:T(8,128)(2,1)} %param.4, f32[464,160]{0,1:T(8,128)S(1)} %select_reduce_fusion, f32[464]{0:T(512)S(1)} %multiply_reduce_fusion, f32[464,160]{0,1:T(8,128)S(1)} %get-tuple-element.6, f32[464]{0:T(512)S(1)} %get-tuple-element.5), kind=kOutput, calls=%fused_computation.1 | convolution fusion | flops 761333760 | bytes 6987392 | tf_op jit(solution)/shard_map/td,te->de/dot_general | solution.py:42
  72.3 3.0 %copy.14 = bf16[5120,160]{1,0:T(8,128)(2,1)S(1)} copy(bf16[5120,160]{0,1:T(8,128)(2,1)} %fusion) | data formatting | bytes 3276800 | tf_op jit(solution)/shard_map/convert_element_type | solution.py:43
  75.3 5.1 %reshape.35 = bf16[16,400,128]{2,1,0:T(8,128)(2,1)} reshape(bf16[5120,160]{1,0:T(8,128)(2,1)S(1)} %copy.14) | data formatting | bytes 3276800 | tf_op jit(solution)/shard_map/reshape | solution.py:43
  80.4 25.7 %all_to_all.31 = bf16[16,400,128]{2,1,0:T(8,128)(2,1)S(1)} all-to-all(bf16[16,400,128]{2,1,0:T(8,128)(2,1)} %reshape.35), channel_id=1, replica_groups=mesh['batch_0'=4,'batch_1'=2,'seq_0'=2,'seq_1'=16,'section'=2] {'batch_0..., dimensions={0} | all-to-all | bytes 3276800 | tf_op jit(solution)/shard_map/all_to_all | solution.py:15
  106.3 23.8 %all_to_all.32 = f32[16,1,3200]{2,1,0:T(1,128)S(1)} all-to-all(f32[16,1,3200]{2,1,0:T(1,128)S(1)} %bitcast.19), channel_id=1, replica_groups=mesh['batch_0'=4,'batch_1'=2,'seq_0'=2,'seq_1'=16,'section'=2] {'seq_1'}, dimensions={0} | all-to-all | bytes 409600 | tf_op jit(solution)/shard_map/all_to_all | solution.py:15
  130.3 0.6 multiply_reduce_fusion.1
  130.9 0.6 broadcast_in_dim_broadcast_in_dim_broadcast_in_dim.6
  131.6 10.8 %all_to_all.33 = f32[16,1,128]{2,1,0:T(1,128)S(1)} all-to-all(f32[16,1,128]{2,1,0:T(1,128)S(1)} %broadcast_in_dim_broadcast_in_dim_broadcast_in_dim.6), channel_id=1, replica_groups=mesh['batch_0'=4,'batch_1'=2,'seq_0'=2,'seq_1'=16,'section'=2] {'batch_0..., dimensions={0} | all-to-all | bytes 16384 | tf_op jit(solution)/shard_map/all_to_all | solution.py:15
  142.4 0.6 slice_reduce_fusion.1
  143.0 0.6 broadcast_in_dim_broadcast_in_dim_broadcast_in_dim.7
  143.6 20.4 %all_to_all.34 = f32[16,1,128]{2,1,0:T(1,128)S(1)} all-to-all(f32[16,1,128]{2,1,0:T(1,128)S(1)} %broadcast_in_dim_broadcast_in_dim_broadcast_in_dim.7), channel_id=1, replica_groups=mesh['batch_0'=4,'batch_1'=2,'seq_0'=2,'seq_1'=16,'section'=2] {'seq_1'}, dimensions={0} | all-to-all | bytes 16384 | tf_op jit(solution)/shard_map/all_to_all | solution.py:15
  164.0 0.6 slice_reduce_fusion
  164.7 6.3 %psum.7 = f32[]{:T(128)} all-reduce(f32[]{:T(128)} %slice_reduce_fusion), channel_id=1, replica_groups=mesh['batch_0'=4,'batch_1'=2,'seq_0'=2,'seq_1'=16,'section'=2] {'section'}, use_global_device_ids=true, to_apply=%region_8.0 | all-reduce | flops 1 | bytes 8 | tf_op jit(solution)/shard_map/psum | solution.py:50
  171.6 0.7 mul.47
  (15 shorter events, 1.3 us)
Async XLA Ops:
  31.0 8.4 %copy-start = (f32[1,464,6]{1,0,2:T(1,128)S(1)}, f32[1,464,6]{1,0,2:T(1,128)}, u32[]{:S(2)}) copy-start(f32[1,464,6]{1,0,2:T(1,128)} %param.5) | copy-start | bytes 33412
  31.1 8.4 %copy-start.1 = (s32[1,464,6]{1,0,2:T(1,128)S(1)}, s32[1,464,6]{1,0,2:T(1,128)}, u32[]{:S(2)}) copy-start(s32[1,464,6]{1,0,2:T(1,128)} %param.6) | copy-start | bytes 33412
  32.6 27.1 %all-to-all-start.1 = ((bf16[16,400,128]{2,1,0:T(8,128)(2,1)}), bf16[16,400,128]{2,1,0:T(8,128)(2,1)}, u32[]{:S(2)}, u32[]{:S(2)}) async-start(bf16[16,400,128]{2,1,0:T(8,128)(2,1)} %broadcast_in_dim.21), calls=%async_computation.1 | async-start | bytes 3276800 | tf_op jit(solution)/shard_map/all_to_all | solution.py:15

commit v2 on v1

v2 whole, which is shorter than its diff:
```python
import functools
import math

import jax
import jax.numpy as jnp
from jax import lax
from jax.experimental import pallas as pl
from jax.experimental.pallas import tpu as pltpu
from jax.sharding import Mesh
from jax.sharding import PartitionSpec as P

BATCH_SEQ = ("batch_0", "batch_1", "seq_0", "seq_1")
PLANE = ("batch_0", "batch_1", "seq_0")
LINE = ("seq_1",)

F32, BF16, I16, I32 = jnp.float32, jnp.bfloat16, jnp.int16, jnp.int32
LANES = 128
WIDE = 160
REST = WIDE - LANES
FOLD = LANES // REST
TOP = 32700.0


def exchanged(parts, axes):
    return lax.all_to_all(parts, axes, split_axis=0, concat_axis=0, tiled=True)


def size(axes):
    return math.prod(lax.axis_size(a) for a in axes)


def exponent_of(biggest):
    return jnp.floor(jnp.log2(TOP / jnp.maximum(biggest, 1e-30)))


def folded(block):
    step = block.shape[0] // FOLD
    rest = [block[step * g : step * (g + 1), LANES:WIDE] for g in range(FOLD)]
    return block[:, :LANES], jnp.concatenate(rest, axis=1)


def spread_kernel(w_ref, out_ref):
    wide, rest = folded(w_ref[...].astype(F32))
    piece = jnp.concatenate([wide, rest], axis=0).astype(BF16)
    out_ref[...] = jnp.broadcast_to(piece[None], out_ref.shape)


def chunk_kernel(rows, p_ref, out_ref, wide, rest):
    pieces = p_ref.shape[0]
    step = rows // FOLD
    group = pieces // FOLD
    for c in range(pieces):
        piece = p_ref[c].astype(F32)
        wide[rows * c : rows * (c + 1), :] = piece[:rows]
        k = c // group
        for g in range(FOLD):
            row = rows * (c % group) + step * g
            rest[row : row + step, REST * k : REST * (k + 1)] = piece[
                rows : rows + step, REST * g : REST * (g + 1)
            ]
    deep = wide.shape[0]
    full = deep + rest.shape[0]
    out_ref[:, :deep, :] = jnp.broadcast_to(
        wide[...].astype(BF16)[None], (out_ref.shape[0], deep, LANES)
    )
    out_ref[:, deep:full, :] = jnp.broadcast_to(
        rest[...].astype(BF16)[None], (out_ref.shape[0], full - deep, LANES)
    )


def layer_kernel(x_hbm, w_ref, c_ref, r_ref, out_ref, x, weight, logits, sems):
    tokens, width = x.shape
    chunks = w_ref.shape[0]
    deep = width // chunks
    block = deep // FOLD
    pairs = chunks // 2
    cols = width // pairs
    copies = [
        pltpu.make_async_copy(
            x_hbm.at[:, cols * j : cols * (j + 1)],
            x.at[:, cols * j : cols * (j + 1)],
            sems.at[j],
        )
        for j in range(pairs)
    ]
    for copy in copies:
        copy.start()
    for g in range(chunks):
        weight[deep * g : deep * (g + 1), :LANES] = w_ref[g, :deep, :]
        rest = w_ref[g, deep : deep + block, :].astype(F32)
        for k in range(FOLD):
            turned = rest if k == 0 else pltpu.roll(rest, LANES - REST * k, axis=1)
            row = deep * g + block * k
            weight[row : row + block, LANES:] = turned.astype(BF16)
    logits[tokens:, :] = jnp.zeros((logits.shape[0] - tokens, logits.shape[1]), F32)
    total = None
    for j in range(pairs):
        copies[j].wait()
        part = jnp.dot(
            x[:, cols * j : cols * (j + 1)],
            weight[cols * j : cols * (j + 1), :],
            preferred_element_type=F32,
        )
        total = part if total is None else total + part
    logits[:tokens, :] = total
    flipped = jnp.transpose(logits[...])[:WIDE, :tokens]
    expo = jnp.exp(flipped)
    probs = expo / jnp.sum(expo, axis=0, keepdims=True)
    expert = lax.broadcasted_iota(I32, (WIDE, tokens), 0)
    d_prob = jnp.zeros((WIDE, tokens), F32)
    for k in range(c_ref.shape[0]):
        d_prob = d_prob + jnp.where(expert == r_ref[k], c_ref[k], 0.0)
    inner = jnp.sum(probs * d_prob, axis=0, keepdims=True)
    d_logits = (probs * (d_prob - inner)).astype(BF16)

    half = WIDE // 2
    left = lax.broadcasted_iota(I32, (WIDE, LANES), 1) < LANES // 2
    row16 = lax.broadcasted_iota(I32, (16, LANES), 0)

    def coded(tile):
        k = exponent_of(jnp.max(jnp.abs(tile), axis=0, keepdims=True))
        return jnp.round(tile * jnp.exp2(k)).astype(I32).astype(I16), k

    def pair(j):
        raw = jnp.dot(d_logits, x[:, cols * j : cols * (j + 1)], preferred_element_type=F32)
        tiles = [raw[:, LANES * i : LANES * (i + 1)] for i in range(5)]
        turned = [None, None] + [pltpu.roll(t, LANES // 2, axis=1) for t in tiles[2:]]
        for odd, (one, two, low, high) in enumerate(
            (
                (tiles[0], tiles[1], tiles[2], turned[2]),
                (
                    jnp.where(left, turned[2], turned[3]),
                    jnp.where(left, turned[3], turned[4]),
                    turned[4],
                    tiles[4],
                ),
            )
        ):
            three = jnp.where(left[:half], low[:half], high[half:])
            one, one_k = coded(one)
            two, two_k = coded(two)
            three, three_k = coded(three)
            g = 2 * j + odd
            out_ref[g, 0:WIDE, :] = one
            out_ref[g, WIDE : 2 * WIDE, :] = two
            out_ref[g, 2 * WIDE : 2 * WIDE + half, :] = three
            keys = jnp.where(row16 == 0, one_k, jnp.where(row16 == 1, two_k, three_k))
            out_ref[g, 2 * WIDE + half :, :] = keys.astype(I32).astype(I16)

    for j in range(pairs):
        pair(j)


def plane_sum_kernel(rows, q_ref, out_ref, table):
    half = WIDE // 2
    base = 2 * WIDE + half
    one = jnp.zeros((WIDE, LANES), F32)
    two = jnp.zeros((WIDE, LANES), F32)
    three = jnp.zeros((half, LANES), F32)
    for s in range(q_ref.shape[0]):
        keys = jnp.exp2(-q_ref[s, base:, :].astype(I32).astype(F32))
        one = one + q_ref[s, :WIDE, :].astype(I32).astype(F32) * keys[0:1]
        two = two + q_ref[s, WIDE : 2 * WIDE, :].astype(I32).astype(F32) * keys[1:2]
        three = three + q_ref[s, 2 * WIDE : base, :].astype(I32).astype(F32) * keys[2:3]
    table[0:LANES, :WIDE] = jnp.transpose(one)
    table[LANES : 2 * LANES, :WIDE] = jnp.transpose(two)
    three = jnp.transpose(three)
    mid = LANES // 2
    table[2 * LANES : 2 * LANES + mid, :WIDE] = jnp.concatenate(
        [three[:mid], three[mid:]], axis=1
    )
    for c in range(out_ref.shape[0]):
        block = table[rows * c : rows * (c + 1), :WIDE]
        k = exponent_of(jnp.max(jnp.abs(block), axis=(0, 1), keepdims=True))
        wide, rest = folded(jnp.round(block * jnp.exp2(k)))
        tail = out_ref.shape[1] - rows - rest.shape[0]
        piece = jnp.concatenate([wide, rest, jnp.broadcast_to(k, (tail, LANES))], axis=0)
        out_ref[c] = piece.astype(I32).astype(I16)


def line_sum_kernel(q_ref, raw_ref, square_ref):
    deep = raw_ref.shape[0]
    raw = jnp.zeros(raw_ref.shape, F32)
    for s in range(q_ref.shape[0]):
        piece = q_ref[s].astype(I32).astype(F32)
        raw = raw + piece[:deep] * jnp.exp2(-piece[deep : deep + 1])
    raw_ref[...] = raw
    square = jnp.sum(raw * raw, axis=(0, 1), keepdims=True)
    square_ref[...] = jnp.broadcast_to(square[None], square_ref.shape)


def again_kernel(s_ref, out_ref):
    out_ref[...] = jnp.broadcast_to(jnp.sum(s_ref[...], axis=0, keepdims=True), out_ref.shape)


def clip_kernel(clip_norm, s_ref, raw_ref, out_ref):
    square = jnp.sum(s_ref[...], axis=0)[:, :1]
    scale = jnp.minimum(1.0, clip_norm / jnp.sqrt(square))
    out = raw_ref[...] * scale
    rows = out_ref.shape[0]
    step = rows // FOLD
    out_ref[:, :LANES] = out[:rows]
    for g in range(FOLD):
        out_ref[step * g : step * (g + 1), LANES:] = out[rows:, REST * g : REST * (g + 1)]


def call(kernel, *args, out, scratch=(), specs=None, name=None):
    vmem = pl.BlockSpec(memory_space=pltpu.VMEM)
    many = isinstance(out, list)
    return pl.pallas_call(
        kernel,
        out_shape=out,
        in_specs=specs or [vmem] * len(args),
        out_specs=[vmem] * len(out) if many else vmem,
        scratch_shapes=list(scratch),
        name=name,
    )(*args)


def shards(acts, cotangent, routes, router_weight):
    tokens, width = acts.shape[1:]
    rows, experts = router_weight.shape[1:]
    plane, line = size(PLANE), size(LINE)
    section = lax.axis_size("section")
    deep = rows * line
    fold_rows = rows + rows // FOLD
    fold_deep = deep + deep // FOLD
    like = jax.ShapeDtypeStruct

    weight = call(
        spread_kernel, router_weight[0], out=like((line, fold_rows, LANES), BF16), name="spread"
    )
    weight = exchanged(weight, LINE)
    weight = call(
        functools.partial(chunk_kernel, rows),
        weight,
        out=like((plane, fold_deep, LANES), BF16),
        scratch=[pltpu.VMEM((deep, LANES), F32), pltpu.VMEM((deep // FOLD, LANES), F32)],
        name="chunk",
    )
    weight = exchanged(weight, PLANE)
    vmem = pl.BlockSpec(memory_space=pltpu.VMEM)
    parts = call(
        layer_kernel,
        acts[0],
        weight,
        jnp.transpose(cotangent, (2, 0, 1)),
        jnp.transpose(routes, (2, 0, 1)),
        specs=[pl.BlockSpec(memory_space=pl.ANY), vmem, vmem, vmem],
        out=like((plane, fold_deep + 16, LANES), I16),
        scratch=[
            pltpu.VMEM((tokens, width), BF16),
            pltpu.VMEM((width, 2 * LANES), BF16),
            pltpu.VMEM((-(-tokens // LANES) * LANES, 2 * LANES), F32),
            pltpu.SemaphoreType.DMA((plane // 2,)),
        ],
        name="layer",
    )
    parts = exchanged(parts, PLANE)
    parts = call(
        functools.partial(plane_sum_kernel, rows),
        parts,
        out=like((line, 32, LANES), I16),
        scratch=[pltpu.VMEM((deep, 2 * LANES), F32)],
        name="plane_sum",
    )
    parts = exchanged(parts, LINE)
    raw, square = call(
        line_sum_kernel,
        parts,
        out=[like((fold_rows, LANES), F32), like((plane * section, 1, LANES), F32)],
        name="line_sum",
    )
    square = exchanged(square, (*PLANE, "section"))
    square = call(again_kernel, square, out=like((line, 1, LANES), F32), name="again")
    square = exchanged(square, LINE)
    clip_norm = 0.25 * math.sqrt(1.0 * section * width * experts)
    out = call(
        functools.partial(clip_kernel, clip_norm),
        square,
        raw,
        out=like((rows, experts), F32),
        name="clip",
    )
    return out[None]


def solution(mesh):
    torus = Mesh(
        mesh.devices.reshape(4, 2, 2, 16, mesh.shape["section"]),
        ("batch_0", "batch_1", "seq_0", "seq_1", "section"),
    )
    placed = P("section", BATCH_SEQ, None)
    return jax.shard_map(
        shards,
        mesh=torus,
        in_specs=(placed, placed, placed, placed),
        out_specs=placed,
        check_vma=False,
    )
```

time: 173 us -> 157 us (0.908)
  Pallas kernels: 0 us -> 21.1 us
  blocking collectives: 114 us -> 134 us
  waiting for transfers between devices: 20 us -> 0 us
  local copies, waits for them, and re-layouts: 17.4 us -> 1.36 us
  matrix products: 8.46 us -> 0 us
  starting transfers between devices: 6.8 us -> 0 us
  other arithmetic: 4.36 us -> 0 us
    all_to_all x5 -> x6, blocking collectives: 108 us -> 134 us  [exchanged(): return lax.all_to_all(parts, axes, split_axis=0, concat_axis=0, tiled=True)]
    pallas_call x0 -> x7, Pallas kernels: none -> 21.1 us  [call(): pl.pallas_call(kernel, out_shape=out, in_specs=specs or [vmem] * len(args...]
    all_to_all x1 -> x0, waiting for transfers between devices: 20 us -> none  [exchanged(): return lax.all_to_all(parts, axes, split_axis=0, concat_axis=0, tiled=True)]
    reshape x2 -> x0, local copies, waits for them, and re-layouts: 9.13 us -> none  [the longest x1 5.13 us: shards(): parts = raw.astype(jnp.bfloat16).reshape(plane, -1, 128)]
    dot_general x2 -> x0, matrix products: 8.46 us -> none  [the longest x1 4.56 us: shards(): jnp.einsum('td,te->de', x, d_logits, preferred_element_type=jnp.float32)]
    all_to_all x1 -> x0, starting transfers between devices: 6.8 us -> none  [exchanged(): return lax.all_to_all(parts, axes, split_axis=0, concat_axis=0, tiled=True)]
    psum x1 -> x0, blocking collectives: 6.26 us -> none  [shards(): squares = lax.psum(squares, 'section')]
    convert_element_type x1 -> x0, local copies, waits for them, and re-layouts: 3.01 us -> none  [shards(): parts = raw.astype(jnp.bfloat16).reshape(plane, -1, 128)]
  transfers between devices with their start and end apart: 1 -> 0, of which waited for: 1 -> 0; matrix products, arithmetic and copies ran while one was open for 0% -> 0% of each run, Pallas kernels for 0% -> 0%
where the time goes in v2:
time: 157 us; the launch traced here: 156 us
  blocking collectives  134 us (85%)
  Pallas kernels  21.1 us (13%)
    all_to_all x6, blocking collectives, exchanged(): return lax.all_to_all(parts, axes, split_axis=0, concat_axis=0, tiled=True)  134 us
    pallas_call x7, Pallas kernels, call(): pl.pallas_call(kernel, out_shape=out, in_specs=specs or [vmem] * len(args...  21.1 us

profile of v2, /device:TPU:1, one launch (start us, length us, event | category | flops | bytes accessed | tf_op | source)
XLA Modules:
  0.0 156.2 jit_solution(17097605888949017523)
XLA Ops:
  0.0 1.4 spread.1
  1.4 27.8 %all_to_all.30.p_ref = bf16[16,25,128]{2,1,0:T(8,128)(2,1)} all-to-all(bf16[16,25,128]{2,1,0:T(8,128)(2,1)} %spread.1), channel_id=1, replica_groups=mesh['batch_0'=4,'batch_1'=2,'seq_0'=2,'seq_1'=16,'section'=2] {'seq_1'}, dimensions={0} | all-to-all | bytes 204800 | tf_op jit(solution)/shard_map/all_to_all | solution.py:25
  29.3 2.3 %chunk.1 = bf16[16,400,128]{2,1,0:T(8,128)(2,1)} custom-call(bf16[16,25,128]{2,1,0:T(8,128)(2,1)} %all_to_all.30.p_ref), custom_call_target="tpu_custom_call" | custom-call | tf_op jit(solution)/shard_map/chunk/pallas_call | solution.py:210
  31.5 26.5 %all_to_all.31.w_ref = bf16[16,400,128]{2,1,0:T(8,128)(2,1)} all-to-all(bf16[16,400,128]{2,1,0:T(8,128)(2,1)} %chunk.1), channel_id=1, replica_groups=mesh['batch_0'=4,'batch_1'=2,'seq_0'=2,'seq_1'=16,'section'=2] {'batch_0..., dimensions={0} | all-to-all | bytes 3276800 | tf_op jit(solution)/shard_map/all_to_all | solution.py:25
  58.1 9.9 %layer.1 = s16[16,416,128]{2,1,0:T(8,128)(2,1)} custom-call(bf16[464,5120]{1,0:T(8,128)(2,1)} %bitcast.5, bf16[16,400,128]{2,1,0:T(8,128)(2,1)} %all_to_all.31.w_ref, f32[6,1,464]{2,1,0:T(1,128)} %bitcast.7, s32[6,1,464]{2,1,0:T(1,128)} %bitcast.8), custom_call_target="tpu_custom_call" | custom-call | tf_op jit(solution)/shard_map/layer/pallas_call | solution.py:210
  68.0 24.0 %all_to_all.32.q_ref = s16[16,416,128]{2,1,0:T(8,128)(2,1)} all-to-all(s16[16,416,128]{2,1,0:T(8,128)(2,1)} %layer.1), channel_id=1, replica_groups=mesh['batch_0'=4,'batch_1'=2,'seq_0'=2,'seq_1'=16,'section'=2] {'batch_0..., dimensions={0} | all-to-all | bytes 3407872 | tf_op jit(solution)/shard_map/all_to_all | solution.py:25
  92.0 2.9 %plane_sum.1 = s16[16,32,128]{2,1,0:T(8,128)(2,1)} custom-call(s16[16,416,128]{2,1,0:T(8,128)(2,1)} %all_to_all.32.q_ref), custom_call_target="tpu_custom_call" | custom-call | tf_op jit(solution)/shard_map/plane_sum/pallas_call | solution.py:210
  95.0 24.4 %all_to_all.33.q_ref = s16[16,32,128]{2,1,0:T(8,128)(2,1)} all-to-all(s16[16,32,128]{2,1,0:T(8,128)(2,1)} %plane_sum.1), channel_id=1, replica_groups=mesh['batch_0'=4,'batch_1'=2,'seq_0'=2,'seq_1'=16,'section'=2] {'seq_1'}, dimensions={0} | all-to-all | bytes 262144 | tf_op jit(solution)/shard_map/all_to_all | solution.py:25
  119.3 1.7 %line_sum.1 = (f32[25,128]{1,0:T(8,128)}, f32[32,1,128]{2,1,0:T(1,128)}) custom-call(s16[16,32,128]{2,1,0:T(8,128)(2,1)} %all_to_all.33.q_ref), custom_call_target="tpu_custom_call" | custom-call | tf_op jit(solution)/shard_map/line_sum/pallas_call | solution.py:210
  121.0 15.9 %all_to_all.34.s_ref = f32[32,1,128]{2,1,0:T(1,128)} all-to-all(f32[32,1,128]{2,1,0:T(1,128)} %get-tuple-element.7), channel_id=1, replica_groups=mesh['batch_0'=4,'batch_1'=2,'seq_0'=2,'seq_1'=16,'section'=2] {'batch_0..., dimensions={0} | all-to-all | bytes 32768 | tf_op jit(solution)/shard_map/all_to_all | solution.py:25
  136.9 1.3 again.1
  138.2 15.1 %all_to_all.35.s_ref = f32[16,1,128]{2,1,0:T(1,128)} all-to-all(f32[16,1,128]{2,1,0:T(1,128)} %again.1), channel_id=1, replica_groups=mesh['batch_0'=4,'batch_1'=2,'seq_0'=2,'seq_1'=16,'section'=2] {'seq_1'}, dimensions={0} | all-to-all | bytes 16384 | tf_op jit(solution)/shard_map/all_to_all | solution.py:25
  153.4 1.5 clip.1
  154.8 1.4 copy.5

commit v3 on v2

--- a/solution.py
+++ b/solution.py
@@ -68,23 +68,13 @@
     )
 
 
-def layer_kernel(x_hbm, w_ref, c_ref, r_ref, out_ref, x, weight, logits, sems):
+def layer_kernel(x, w_ref, c_ref, r_ref, out_ref, weight, logits):
     tokens, width = x.shape
     chunks = w_ref.shape[0]
     deep = width // chunks
     block = deep // FOLD
     pairs = chunks // 2
     cols = width // pairs
-    copies = [
-        pltpu.make_async_copy(
-            x_hbm.at[:, cols * j : cols * (j + 1)],
-            x.at[:, cols * j : cols * (j + 1)],
-            sems.at[j],
-        )
-        for j in range(pairs)
-    ]
-    for copy in copies:
-        copy.start()
     for g in range(chunks):
         weight[deep * g : deep * (g + 1), :LANES] = w_ref[g, :deep, :]
         rest = w_ref[g, deep : deep + block, :].astype(F32)
@@ -95,7 +85,6 @@
     logits[tokens:, :] = jnp.zeros((logits.shape[0] - tokens, logits.shape[1]), F32)
     total = None
     for j in range(pairs):
-        copies[j].wait()
         part = jnp.dot(
             x[:, cols * j : cols * (j + 1)],
             weight[cols * j : cols * (j + 1), :],
@@ -199,20 +188,21 @@
     out = raw_ref[...] * scale
     rows = out_ref.shape[0]
     step = rows // FOLD
-    out_ref[:, :LANES] = out[:rows]
+    out_ref[:, 0, :LANES] = out[:rows]
     for g in range(FOLD):
-        out_ref[step * g : step * (g + 1), LANES:] = out[rows:, REST * g : REST * (g + 1)]
-
-
-def call(kernel, *args, out, scratch=(), specs=None, name=None):
+        out_ref[step * g : step * (g + 1), 0, LANES:] = out[rows:, REST * g : REST * (g + 1)]
+
+
+def call(kernel, *args, out, mib, scratch=(), name=None):
     vmem = pl.BlockSpec(memory_space=pltpu.VMEM)
     many = isinstance(out, list)
     return pl.pallas_call(
         kernel,
         out_shape=out,
-        in_specs=specs or [vmem] * len(args),
+        in_specs=[vmem] * len(args),
         out_specs=[vmem] * len(out) if many else vmem,
         scratch_shapes=list(scratch),
+        compiler_params=pltpu.CompilerParams(vmem_limit_bytes=mib << 20),
         name=name,
     )(*args)
 
@@ -228,7 +218,7 @@
     like = jax.ShapeDtypeStruct
 
     weight = call(
-        spread_kernel, router_weight[0], out=like((line, fold_rows, LANES), BF16), name="spread"
+        spread_kernel, router_weight[0], out=like((line, fold_rows, LANES), BF16), mib=2, name="spread"
     )
     weight = exchanged(weight, LINE)
     weight = call(
@@ -236,25 +226,21 @@
         weight,
         out=like((plane, fold_deep, LANES), BF16),
         scratch=[pltpu.VMEM((deep, LANES), F32), pltpu.VMEM((deep // FOLD, LANES), F32)],
-        name="chunk",
+        mib=4, name="chunk",
     )
     weight = exchanged(weight, PLANE)
-    vmem = pl.BlockSpec(memory_space=pltpu.VMEM)
     parts = call(
         layer_kernel,
         acts[0],
         weight,
         jnp.transpose(cotangent, (2, 0, 1)),
         jnp.transpose(routes, (2, 0, 1)),
-        specs=[pl.BlockSpec(memory_space=pl.ANY), vmem, vmem, vmem],
         out=like((plane, fold_deep + 16, LANES), I16),
         scratch=[
-            pltpu.VMEM((tokens, width), BF16),
             pltpu.VMEM((width, 2 * LANES), BF16),
             pltpu.VMEM((-(-tokens // LANES) * LANES, 2 * LANES), F32),
-            pltpu.SemaphoreType.DMA((plane // 2,)),
         ],
-        name="layer",
+        mib=20, name="layer",
     )
     parts = exchanged(parts, PLANE)
     parts = call(
@@ -262,27 +248,27 @@
         parts,
         out=like((line, 32, LANES), I16),
         scratch=[pltpu.VMEM((deep, 2 * LANES), F32)],
-        name="plane_sum",
+        mib=6, name="plane_sum",
     )
     parts = exchanged(parts, LINE)
     raw, square = call(
         line_sum_kernel,
         parts,
         out=[like((fold_rows, LANES), F32), like((plane * section, 1, LANES), F32)],
-        name="line_sum",
+        mib=2, name="line_sum",
     )
     square = exchanged(square, (*PLANE, "section"))
-    square = call(again_kernel, square, out=like((line, 1, LANES), F32), name="again")
+    square = call(again_kernel, square, out=like((line, 1, LANES), F32), mib=1, name="again")
     square = exchanged(square, LINE)
     clip_norm = 0.25 * math.sqrt(1.0 * section * width * experts)
     out = call(
         functools.partial(clip_kernel, clip_norm),
         square,
         raw,
-        out=like((rows, experts), F32),
-        name="clip",
-    )
-    return out[None]
+        out=like((rows, 1, experts), F32),
+        mib=1, name="clip",
+    )
+    return jnp.transpose(out, (1, 0, 2))
 
 
 def solution(mesh):

time: 157 us -> 140 us (0.89)
  Pallas kernels: 21.1 us -> 7.45 us
  blocking collectives: 134 us -> 131 us
    pallas_call x7, Pallas kernels: 21.1 us -> 7.45 us  [call(): pl.pallas_call(kernel, out_shape=out, in_specs=[vmem] * len(args), out_sp...]
    all_to_all x6, blocking collectives: 134 us -> 131 us  [exchanged(): return lax.all_to_all(parts, axes, split_axis=0, concat_axis=0, tiled=True)]
where the time goes in v3:
time: 140 us; the launch traced here: 139 us
  blocking collectives  131 us (94%)
  Pallas kernels  7.45 us (5%)
    all_to_all x6, blocking collectives, exchanged(): return lax.all_to_all(parts, axes, split_axis=0, concat_axis=0, tiled=True)  131 us
    pallas_call x7, Pallas kernels, call(): pl.pallas_call(kernel, out_shape=out, in_specs=[vmem] * len(args), out_sp...  7.45 us

profile of v3, /device:TPU:1, one launch (start us, length us, event | category | flops | bytes accessed | tf_op | source)
XLA Modules:
  0.0 139.4 jit_solution(6874893925572985034)
XLA Ops:
  0.0 0.0 copy-start.3
  0.0 0.7 copy-done.3
  0.7 0.1 spread.1
  0.8 27.5 %all_to_all.30.p_ref = bf16[16,25,128]{2,1,0:T(8,128)(2,1)S(1)} all-to-all(bf16[16,25,128]{2,1,0:T(8,128)(2,1)S(1)} %spread.1), channel_id=1, replica_groups=mesh['batch_0'=4,'batch_1'=2,'seq_0'=2,'seq_1'=16,'section'=2] {'seq_1'}, dimensions={0} | all-to-all | bytes 204800 | tf_op jit(solution)/shard_map/all_to_all | solution.py:25
  28.3 0.0 copy-start
  28.3 0.2 chunk.1
  28.5 0.0 copy-start.1
  28.5 0.0 copy-start.2
  28.5 26.5 %all_to_all.31.w_ref = bf16[16,400,128]{2,1,0:T(8,128)(2,1)S(1)} all-to-all(bf16[16,400,128]{2,1,0:T(8,128)(2,1)S(1)} %chunk.1), channel_id=1, replica_groups=mesh['batch_0'=4,'batch_1'=2,'seq_0'=2,'seq_1'=16,'section'=2] {'batch_0..., dimensions={0} | all-to-all | bytes 3276800 | tf_op jit(solution)/shard_map/all_to_all | solution.py:25
  55.0 0.0 copy-done
  55.0 0.0 copy-done.1
  55.0 0.0 copy-done.2
  55.0 5.4 %layer.1 = s16[16,416,128]{2,1,0:T(8,128)(2,1)S(1)} custom-call(bf16[464,5120]{1,0:T(8,128)(2,1)S(1)} %bitcast.5, bf16[16,400,128]{2,1,0:T(8,128)(2,1)S(1)} %all_to_all.31.w_ref, f32[6,1,464]{2,1,0:T(1,128)S(1)} %bitcast.6, s32[6,1,464]{2,1,0:T(1,128)S(1)} %bitcast.7), custom_call_target="tpu_custom_call" | custom-call | tf_op jit(solution)/shard_map/layer/pallas_call | solution.py:199
  60.4 22.8 %all_to_all.32.q_ref = s16[16,416,128]{2,1,0:T(8,128)(2,1)S(1)} all-to-all(s16[16,416,128]{2,1,0:T(8,128)(2,1)S(1)} %layer.1), channel_id=1, replica_groups=mesh['batch_0'=4,'batch_1'=2,'seq_0'=2,'seq_1'=16,'section'=2] {'batch_0..., dimensions={0} | all-to-all | bytes 3407872 | tf_op jit(solution)/shard_map/all_to_all | solution.py:25
  83.3 0.8 plane_sum.1
  84.1 25.3 %all_to_all.33.q_ref = s16[16,32,128]{2,1,0:T(8,128)(2,1)S(1)} all-to-all(s16[16,32,128]{2,1,0:T(8,128)(2,1)S(1)} %plane_sum.1), channel_id=1, replica_groups=mesh['batch_0'=4,'batch_1'=2,'seq_0'=2,'seq_1'=16,'section'=2] {'seq_1'}, dimensions={0} | all-to-all | bytes 262144 | tf_op jit(solution)/shard_map/all_to_all | solution.py:25
  109.4 0.2 line_sum.1
  109.5 14.7 %all_to_all.34.s_ref = f32[32,1,128]{2,1,0:T(1,128)S(1)} all-to-all(f32[32,1,128]{2,1,0:T(1,128)S(1)} %get-tuple-element.7), channel_id=1, replica_groups=mesh['batch_0'=4,'batch_1'=2,'seq_0'=2,'seq_1'=16,'section'=2] {'batch_0..., dimensions={0} | all-to-all | bytes 32768 | tf_op jit(solution)/shard_map/all_to_all | solution.py:25
  124.3 14.3 %all_to_all.35.s_ref = f32[16,1,128]{2,1,0:T(1,128)S(1)} all-to-all(f32[16,1,128]{2,1,0:T(1,128)S(1)} %again.1), channel_id=1, replica_groups=mesh['batch_0'=4,'batch_1'=2,'seq_0'=2,'seq_1'=16,'section'=2] {'seq_1'}, dimensions={0} | all-to-all | bytes 16384 | tf_op jit(solution)/shard_map/all_to_all | solution.py:25
  138.6 0.8 clip.1
  (1 shorter events, 0.0 us)
Async XLA Ops:
  0.0 0.7 copy-start.3
  28.3 26.7 %copy-start = (bf16[1,464,5120]{2,1,0:T(8,128)(2,1)S(1)}, bf16[1,464,5120]{2,1,0:T(8,128)(2,1)}, u32[]{:S(2)}) copy-start(bf16[1,464,5120]{2,1,0:T(8,128)(2,1)} %param.4) | copy-start | bytes 14254084
  28.5 26.5 %copy-start.1 = (f32[1,464,6]{1,0,2:T(1,128)S(1)}, f32[1,464,6]{1,0,2:T(1,128)}, u32[]{:S(2)}) copy-start(f32[1,464,6]{1,0,2:T(1,128)} %param.5) | copy-start | bytes 33412
  28.5 26.5 %copy-start.2 = (s32[1,464,6]{1,0,2:T(1,128)S(1)}, s32[1,464,6]{1,0,2:T(1,128)}, u32[]{:S(2)}) copy-start(s32[1,464,6]{1,0,2:T(1,128)} %param.6) | copy-start | bytes 33412

commit v4 on v3

--- a/solution.py
+++ b/solution.py
@@ -3,6 +3,7 @@
 
 import jax
 import jax.numpy as jnp
+import numpy as np
 from jax import lax
 from jax.experimental import pallas as pl
 from jax.experimental.pallas import tpu as pltpu
@@ -12,6 +13,7 @@
 BATCH_SEQ = ("batch_0", "batch_1", "seq_0", "seq_1")
 PLANE = ("batch_0", "batch_1", "seq_0")
 LINE = ("seq_1",)
+EVERY = BATCH_SEQ + ("section",)
 
 F32, BF16, I16, I32 = jnp.float32, jnp.bfloat16, jnp.int16, jnp.int32
 LANES = 128
@@ -19,14 +21,49 @@
 REST = WIDE - LANES
 FOLD = LANES // REST
 TOP = 32700.0
-
-
-def exchanged(parts, axes):
-    return lax.all_to_all(parts, axes, split_axis=0, concat_axis=0, tiled=True)
+LAG = 13000
 
 
 def size(axes):
     return math.prod(lax.axis_size(a) for a in axes)
+
+
+def ids():
+    sizes = [lax.axis_size(a) for a in EVERY]
+    index = np.arange(math.prod(sizes)).reshape(sizes)
+    for axis, name in enumerate(EVERY):
+        if name != "batch_1":
+            index = np.roll(index, -(sizes[axis] // 2), axis=axis)
+    return index.reshape(size(PLANE), size(LINE), 2)
+
+
+def plane_order():
+    row, near, far = (lax.axis_size(a) for a in PLANE)
+    index = np.arange(row * near * far).reshape(row, near, far)
+    return np.roll(index, (-(row // 2), -(far // 2)), axis=(0, 2)).ravel().tolist()
+
+
+def line_order():
+    line = size(LINE)
+    return np.roll(np.arange(line), -(line // 2)).tolist()
+
+
+def exchanged(parts, groups):
+    return lax.all_to_all(
+        parts, EVERY, split_axis=0, concat_axis=0, axis_index_groups=groups.tolist(), tiled=True
+    )
+
+
+def over_plane(parts):
+    return exchanged(parts, np.moveaxis(ids(), 0, -1).reshape(-1, size(PLANE)))
+
+
+def over_line(parts):
+    return exchanged(parts, np.moveaxis(ids(), 1, -1).reshape(-1, size(LINE)))
+
+
+def over_plane_and_section(parts):
+    return exchanged(parts, ids().transpose(1, 2, 0).reshape(size(LINE), -1))
 
 
 def exponent_of(biggest):
@@ -40,17 +77,21 @@
 
 
 def spread_kernel(w_ref, out_ref):
+    @pl.when(lax.axis_index("section") == 1)
+    def _():
+        pl.delay(LAG)
+
     wide, rest = folded(w_ref[...].astype(F32))
     piece = jnp.concatenate([wide, rest], axis=0).astype(BF16)
     out_ref[...] = jnp.broadcast_to(piece[None], out_ref.shape)
 
 
-def chunk_kernel(rows, p_ref, out_ref, wide, rest):
+def chunk_kernel(rows, order, p_ref, out_ref, wide, rest):
     pieces = p_ref.shape[0]
     step = rows // FOLD
     group = pieces // FOLD
     for c in range(pieces):
-        piece = p_ref[c].astype(F32)
+        piece = p_ref[order.index(c)].astype(F32)
         wide[rows * c : rows * (c + 1), :] = piece[:rows]
         k = c // group
         for g in range(FOLD):
@@ -68,7 +109,7 @@
     )
 
 
-def layer_kernel(x, w_ref, c_ref, r_ref, out_ref, weight, logits):
+def layer_kernel(order, x, w_ref, c_ref, r_ref, out_ref, weight, logits):
     tokens, width = x.shape
     chunks = w_ref.shape[0]
     deep = width // chunks
@@ -76,8 +117,8 @@
     pairs = chunks // 2
     cols = width // pairs
     for g in range(chunks):
-        weight[deep * g : deep * (g + 1), :LANES] = w_ref[g, :deep, :]
-        rest = w_ref[g, deep : deep + block, :].astype(F32)
+        weight[deep * g : deep * (g + 1), :LANES] = w_ref[order.index(g), :deep, :]
+        rest = w_ref[order.index(g), deep : deep + block, :].astype(F32)
         for k in range(FOLD):
             turned = rest if k == 0 else pltpu.roll(rest, LANES - REST * k, axis=1)
             row = deep * g + block * k
@@ -129,7 +170,7 @@
             one, one_k = coded(one)
             two, two_k = coded(two)
             three, three_k = coded(three)
-            g = 2 * j + odd
+            g = order.index(2 * j + odd)
             out_ref[g, 0:WIDE, :] = one
             out_ref[g, WIDE : 2 * WIDE, :] = two
             out_ref[g, 2 * WIDE : 2 * WIDE + half, :] = three
@@ -140,7 +181,7 @@
         pair(j)
 
 
-def plane_sum_kernel(rows, q_ref, out_ref, table):
+def plane_sum_kernel(rows, order, q_ref, out_ref, table):
     half = WIDE // 2
     base = 2 * WIDE + half
     one = jnp.zeros((WIDE, LANES), F32)
@@ -164,7 +205,7 @@
         wide, rest = folded(jnp.round(block * jnp.exp2(k)))
         tail = out_ref.shape[1] - rows - rest.shape[0]
         piece = jnp.concatenate([wide, rest, jnp.broadcast_to(k, (tail, LANES))], axis=0)
-        out_ref[c] = piece.astype(I32).astype(I16)
+        out_ref[order.index(c)] = piece.astype(I32).astype(I16)
 
 
 def line_sum_kernel(q_ref, raw_ref, square_ref):
@@ -220,17 +261,17 @@
     weight = call(
         spread_kernel, router_weight[0], out=like((line, fold_rows, LANES), BF16), mib=2, name="spread"
     )
-    weight = exchanged(weight, LINE)
+    weight = over_line(weight)
     weight = call(
-        functools.partial(chunk_kernel, rows),
+        functools.partial(chunk_kernel, rows, line_order()),
         weight,
         out=like((plane, fold_deep, LANES), BF16),
         scratch=[pltpu.VMEM((deep, LANES), F32), pltpu.VMEM((deep // FOLD, LANES), F32)],
         mib=4, name="chunk",
     )
-    weight = exchanged(weight, PLANE)
+    weight = over_plane(weight)
     parts = call(
-        layer_kernel,
+        functools.partial(layer_kernel, plane_order()),
         acts[0],
         weight,
         jnp.transpose(cotangent, (2, 0, 1)),
@@ -242,24 +283,24 @@
         ],
         mib=20, name="layer",
     )
-    parts = exchanged(parts, PLANE)
+    parts = over_plane(parts)
     parts = call(
-        functools.partial(plane_sum_kernel, rows),
+        functools.partial(plane_sum_kernel, rows, line_order()),
         parts,
         out=like((line, 32, LANES), I16),
         scratch=[pltpu.VMEM((deep, 2 * LANES), F32)],
         mib=6, name="plane_sum",
     )
-    parts = exchanged(parts, LINE)
+    parts = over_line(parts)
     raw, square = call(
         line_sum_kernel,
         parts,
         out=[like((fold_rows, LANES), F32), like((plane * section, 1, LANES), F32)],
         mib=2, name="line_sum",
     )
-    square = exchanged(square, (*PLANE, "section"))
+    square = over_plane_and_section(square)
     square = call(again_kernel, square, out=like((line, 1, LANES), F32), mib=1, name="again")
-    square = exchanged(square, LINE)
+    square = over_line(square)
     clip_norm = 0.25 * math.sqrt(1.0 * section * width * experts)
     out = call(
         functools.partial(clip_kernel, clip_norm),

time: 140 us -> 121 us (0.86)
  blocking collectives: 131 us -> 98.6 us
  Pallas kernels: 7.45 us -> 20.4 us
    all_to_all x6, blocking collectives: 131 us -> 98.6 us  [exchanged(): lax.all_to_all(parts, EVERY, split_axis=0, concat_axis=0, axis_index_grou...]
    pallas_call x7, Pallas kernels: 7.45 us -> 20.4 us  [call(): pl.pallas_call(kernel, out_shape=out, in_specs=[vmem] * len(args), out_sp...]
where the time goes in v4:
time: 121 us; the launch traced here: 120 us
  blocking collectives  98.6 us (81%)
  Pallas kernels  20.4 us (17%)
    all_to_all x6, blocking collectives, exchanged(): lax.all_to_all(parts, EVERY, split_axis=0, concat_axis=0, axis_index_grou...  98.6 us
    pallas_call x7, Pallas kernels, call(): pl.pallas_call(kernel, out_shape=out, in_specs=[vmem] * len(args), out_sp...  20.4 us

profile of v4, /device:TPU:1, one launch (start us, length us, event | category | flops | bytes accessed | tf_op | source)
XLA Modules:
  0.0 119.8 jit_solution(17973423191123190113)
XLA Ops:
  0.0 0.0 copy-start.3
  0.0 0.7 copy-done.3
  0.7 13.1 %spread.1 = bf16[16,25,128]{2,1,0:T(8,128)(2,1)S(1)} custom-call(bf16[20,160]{1,0:T(8,128)(2,1)S(1)} %bitcast.8), custom_call_target="tpu_custom_call" | custom-call | tf_op jit(solution)/shard_map/spread/pallas_call | solution.py:240
  13.8 23.4 %all_to_all.30.p_ref = bf16[16,25,128]{2,1,0:T(8,128)(2,1)S(1)} all-to-all(bf16[16,25,128]{2,1,0:T(8,128)(2,1)S(1)} %spread.1), channel_id=1, replica_groups={{305,307,309,311,313,315,317,319,289,291,293,295,297,299,301,303},{304,..., dimensions={0} | all-to-all | bytes 204800 | tf_op jit(solution)/shard_map/all_to_all | solution.py:52
  37.2 0.0 copy-start
  37.2 0.2 chunk.1
  37.4 0.0 copy-start.1
  37.4 0.0 copy-start.2
  37.5 19.0 %all_to_all.31.w_ref = bf16[16,400,128]{2,1,0:T(8,128)(2,1)S(1)} all-to-all(bf16[16,400,128]{2,1,0:T(8,128)(2,1)S(1)} %chunk.1), channel_id=1, replica_groups={{305,273,369,337,433,401,497,465,49,17,113,81,177,145,241,209},{304,272..., dimensions={0} | all-to-all | bytes 3276800 | tf_op jit(solution)/shard_map/all_to_all | solution.py:52
  56.4 0.0 copy-done
  56.4 0.0 copy-done.1
  56.4 0.0 copy-done.2
  56.4 5.4 %layer.1 = s16[16,416,128]{2,1,0:T(8,128)(2,1)S(1)} custom-call(bf16[464,5120]{1,0:T(8,128)(2,1)S(1)} %bitcast.5, bf16[16,400,128]{2,1,0:T(8,128)(2,1)S(1)} %all_to_all.31.w_ref, f32[6,1,464]{2,1,0:T(1,128)S(1)} %bitcast.6, s32[6,1,464]{2,1,0:T(1,128)S(1)} %bitcast.7), custom_call_target="tpu_custom_call" | custom-call | tf_op jit(solution)/shard_map/layer/pallas_call | solution.py:240
  61.8 18.0 %all_to_all.32.q_ref = s16[16,416,128]{2,1,0:T(8,128)(2,1)S(1)} all-to-all(s16[16,416,128]{2,1,0:T(8,128)(2,1)S(1)} %layer.1), channel_id=1, replica_groups={{305,273,369,337,433,401,497,465,49,17,113,81,177,145,241,209},{304,272..., dimensions={0} | all-to-all | bytes 3407872 | tf_op jit(solution)/shard_map/all_to_all | solution.py:52
  79.9 0.8 plane_sum.1
  80.7 15.5 %all_to_all.33.q_ref = s16[16,32,128]{2,1,0:T(8,128)(2,1)S(1)} all-to-all(s16[16,32,128]{2,1,0:T(8,128)(2,1)S(1)} %plane_sum.1), channel_id=1, replica_groups={{305,307,309,311,313,315,317,319,289,291,293,295,297,299,301,303},{304,..., dimensions={0} | all-to-all | bytes 262144 | tf_op jit(solution)/shard_map/all_to_all | solution.py:52
  96.2 0.2 line_sum.1
  96.4 9.8 %all_to_all.34.s_ref = f32[32,1,128]{2,1,0:T(1,128)S(1)} all-to-all(f32[32,1,128]{2,1,0:T(1,128)S(1)} %get-tuple-element.7), channel_id=1, replica_groups={{305,273,369,337,433,401,497,465,49,17,113,81,177,145,241,209,304,272,3..., dimensions={0} | all-to-all | bytes 32768 | tf_op jit(solution)/shard_map/all_to_all | solution.py:52
  106.2 12.8 %all_to_all.35.s_ref = f32[16,1,128]{2,1,0:T(1,128)S(1)} all-to-all(f32[16,1,128]{2,1,0:T(1,128)S(1)} %again.1), channel_id=1, replica_groups={{305,307,309,311,313,315,317,319,289,291,293,295,297,299,301,303},{304,..., dimensions={0} | all-to-all | bytes 16384 | tf_op jit(solution)/shard_map/all_to_all | solution.py:52
  119.1 0.8 clip.1
  (1 shorter events, 0.0 us)
Async XLA Ops:
  0.0 0.7 copy-start.3
  37.2 19.2 %copy-start = (bf16[1,464,5120]{2,1,0:T(8,128)(2,1)S(1)}, bf16[1,464,5120]{2,1,0:T(8,128)(2,1)}, u32[]{:S(2)}) copy-start(bf16[1,464,5120]{2,1,0:T(8,128)(2,1)} %param.4) | copy-start | bytes 14254084
  37.4 19.0 %copy-start.1 = (f32[1,464,6]{1,0,2:T(1,128)S(1)}, f32[1,464,6]{1,0,2:T(1,128)}, u32[]{:S(2)}) copy-start(f32[1,464,6]{1,0,2:T(1,128)} %param.5) | copy-start | bytes 33412
  37.4 19.0 %copy-start.2 = (s32[1,464,6]{1,0,2:T(1,128)S(1)}, s32[1,464,6]{1,0,2:T(1,128)}, u32[]{:S(2)}) copy-start(s32[1,464,6]{1,0,2:T(1,128)} %param.6) | copy-start | bytes 33412

commit v5 on v4

--- a/solution.py
+++ b/solution.py
@@ -21,7 +21,7 @@
 REST = WIDE - LANES
 FOLD = LANES // REST
 TOP = 32700.0
-LAG = 13000
+LAG = 6500
 
 
 def size(axes):
@@ -77,7 +77,7 @@
 
 
 def spread_kernel(w_ref, out_ref):
-    @pl.when(lax.axis_index("section") == 1)
+    @pl.when(lax.axis_index("section") == 0)
     def _():
         pl.delay(LAG)
 
@@ -124,14 +124,7 @@
             row = deep * g + block * k
             weight[row : row + block, LANES:] = turned.astype(BF16)
     logits[tokens:, :] = jnp.zeros((logits.shape[0] - tokens, logits.shape[1]), F32)
-    total = None
-    for j in range(pairs):
-        part = jnp.dot(
-            x[:, cols * j : cols * (j + 1)],
-            weight[cols * j : cols * (j + 1), :],
-            preferred_element_type=F32,
-        )
-        total = part if total is None else total + part
+    total = jnp.dot(x[...], weight[...], preferred_element_type=F32)
     logits[:tokens, :] = total
     flipped = jnp.transpose(logits[...])[:WIDE, :tokens]
     expo = jnp.exp(flipped)

time: 121 us -> 119 us (0.983)
  Pallas kernels: 20.4 us -> 7.23 us
  blocking collectives: 98.6 us -> 110 us
    pallas_call x7, Pallas kernels: 20.4 us -> 7.23 us  [call(): pl.pallas_call(kernel, out_shape=out, in_specs=[vmem] * len(args), out_sp...]
    all_to_all x6, blocking collectives: 98.6 us -> 110 us  [exchanged(): lax.all_to_all(parts, EVERY, split_axis=0, concat_axis=0, axis_index_grou...]
where the time goes in v5:
time: 119 us; the launch traced here: 118 us
  blocking collectives  110 us (92%)
  Pallas kernels  7.23 us (6%)
    all_to_all x6, blocking collectives, exchanged(): lax.all_to_all(parts, EVERY, split_axis=0, concat_axis=0, axis_index_grou...  110 us
    pallas_call x7, Pallas kernels, call(): pl.pallas_call(kernel, out_shape=out, in_specs=[vmem] * len(args), out_sp...  7.23 us

profile of v5, /device:TPU:1, one launch (start us, length us, event | category | flops | bytes accessed | tf_op | source)
XLA Modules:
  0.0 118.0 jit_solution(4855881221525677740)
XLA Ops:
  0.0 0.0 copy-start.3
  0.0 0.7 copy-done.3
  0.7 0.1 spread.1
  0.8 23.1 %all_to_all.30.p_ref = bf16[16,25,128]{2,1,0:T(8,128)(2,1)S(1)} all-to-all(bf16[16,25,128]{2,1,0:T(8,128)(2,1)S(1)} %spread.1), channel_id=1, replica_groups={{305,307,309,311,313,315,317,319,289,291,293,295,297,299,301,303},{304,..., dimensions={0} | all-to-all | bytes 204800 | tf_op jit(solution)/shard_map/all_to_all | solution.py:52
  23.9 0.0 copy-start
  23.9 0.2 chunk.1
  24.1 0.0 copy-start.1
  24.1 0.0 copy-start.2
  24.2 19.0 %all_to_all.31.w_ref = bf16[16,400,128]{2,1,0:T(8,128)(2,1)S(1)} all-to-all(bf16[16,400,128]{2,1,0:T(8,128)(2,1)S(1)} %chunk.1), channel_id=1, replica_groups={{305,273,369,337,433,401,497,465,49,17,113,81,177,145,241,209},{304,272..., dimensions={0} | all-to-all | bytes 3276800 | tf_op jit(solution)/shard_map/all_to_all | solution.py:52
  43.1 0.0 copy-done
  43.1 0.0 copy-done.1
  43.1 0.0 copy-done.2
  43.1 5.2 %layer.1 = s16[16,416,128]{2,1,0:T(8,128)(2,1)S(1)} custom-call(bf16[464,5120]{1,0:T(8,128)(2,1)S(1)} %bitcast.5, bf16[16,400,128]{2,1,0:T(8,128)(2,1)S(1)} %all_to_all.31.w_ref, f32[6,1,464]{2,1,0:T(1,128)S(1)} %bitcast.6, s32[6,1,464]{2,1,0:T(1,128)S(1)} %bitcast.7), custom_call_target="tpu_custom_call" | custom-call | tf_op jit(solution)/shard_map/layer/pallas_call | solution.py:233
  48.3 18.1 %all_to_all.32.q_ref = s16[16,416,128]{2,1,0:T(8,128)(2,1)S(1)} all-to-all(s16[16,416,128]{2,1,0:T(8,128)(2,1)S(1)} %layer.1), channel_id=1, replica_groups={{305,273,369,337,433,401,497,465,49,17,113,81,177,145,241,209},{304,272..., dimensions={0} | all-to-all | bytes 3407872 | tf_op jit(solution)/shard_map/all_to_all | solution.py:52
  66.5 0.8 plane_sum.1
  67.3 15.8 %all_to_all.33.q_ref = s16[16,32,128]{2,1,0:T(8,128)(2,1)S(1)} all-to-all(s16[16,32,128]{2,1,0:T(8,128)(2,1)S(1)} %plane_sum.1), channel_id=1, replica_groups={{305,307,309,311,313,315,317,319,289,291,293,295,297,299,301,303},{304,..., dimensions={0} | all-to-all | bytes 262144 | tf_op jit(solution)/shard_map/all_to_all | solution.py:52
  83.1 0.2 line_sum.1
  83.3 21.1 %all_to_all.34.s_ref = f32[32,1,128]{2,1,0:T(1,128)S(1)} all-to-all(f32[32,1,128]{2,1,0:T(1,128)S(1)} %get-tuple-element.7), channel_id=1, replica_groups={{305,273,369,337,433,401,497,465,49,17,113,81,177,145,241,209,304,272,3..., dimensions={0} | all-to-all | bytes 32768 | tf_op jit(solution)/shard_map/all_to_all | solution.py:52
  104.4 12.8 %all_to_all.35.s_ref = f32[16,1,128]{2,1,0:T(1,128)S(1)} all-to-all(f32[16,1,128]{2,1,0:T(1,128)S(1)} %again.1), channel_id=1, replica_groups={{305,307,309,311,313,315,317,319,289,291,293,295,297,299,301,303},{304,..., dimensions={0} | all-to-all | bytes 16384 | tf_op jit(solution)/shard_map/all_to_all | solution.py:52
  117.2 0.8 clip.1
  (1 shorter events, 0.0 us)
Async XLA Ops:
  0.0 0.7 copy-start.3
  23.9 19.2 %copy-start = (bf16[1,464,5120]{2,1,0:T(8,128)(2,1)S(1)}, bf16[1,464,5120]{2,1,0:T(8,128)(2,1)}, u32[]{:S(2)}) copy-start(bf16[1,464,5120]{2,1,0:T(8,128)(2,1)} %param.4) | copy-start | bytes 14254084
  24.1 19.0 %copy-start.1 = (f32[1,464,6]{1,0,2:T(1,128)S(1)}, f32[1,464,6]{1,0,2:T(1,128)}, u32[]{:S(2)}) copy-start(f32[1,464,6]{1,0,2:T(1,128)} %param.5) | copy-start | bytes 33412
  24.1 19.0 %copy-start.2 = (s32[1,464,6]{1,0,2:T(1,128)S(1)}, s32[1,464,6]{1,0,2:T(1,128)}, u32[]{:S(2)}) copy-start(s32[1,464,6]{1,0,2:T(1,128)} %param.6) | copy-start | bytes 33412

commit v6 on v5

--- a/solution.py
+++ b/solution.py
@@ -138,7 +138,7 @@
 
     half = WIDE // 2
     left = lax.broadcasted_iota(I32, (WIDE, LANES), 1) < LANES // 2
-    row16 = lax.broadcasted_iota(I32, (16, LANES), 0)
+    row8 = lax.broadcasted_iota(I32, (8, LANES), 0)
 
     def coded(tile):
         k = exponent_of(jnp.max(jnp.abs(tile), axis=0, keepdims=True))
@@ -167,7 +167,7 @@
             out_ref[g, 0:WIDE, :] = one
             out_ref[g, WIDE : 2 * WIDE, :] = two
             out_ref[g, 2 * WIDE : 2 * WIDE + half, :] = three
-            keys = jnp.where(row16 == 0, one_k, jnp.where(row16 == 1, two_k, three_k))
+            keys = jnp.where(row8 == 0, one_k, jnp.where(row8 == 1, two_k, three_k))
             out_ref[g, 2 * WIDE + half :, :] = keys.astype(I32).astype(I16)
 
     for j in range(pairs):
@@ -269,7 +269,7 @@
         weight,
         jnp.transpose(cotangent, (2, 0, 1)),
         jnp.transpose(routes, (2, 0, 1)),
-        out=like((plane, fold_deep + 16, LANES), I16),
+        out=like((plane, fold_deep + 8, LANES), I16),
         scratch=[
             pltpu.VMEM((width, 2 * LANES), BF16),
             pltpu.VMEM((-(-tokens // LANES) * LANES, 2 * LANES), F32),

time: 119 us -> 119 us (level)
  no operation moved by 1% of the time
where the time goes in v6:
time: 119 us; the launch traced here: 118 us
  blocking collectives  110 us (92%)
  Pallas kernels  7.22 us (6%)
    all_to_all x6, blocking collectives, exchanged(): lax.all_to_all(parts, EVERY, split_axis=0, concat_axis=0, axis_index_grou...  110 us
    pallas_call x7, Pallas kernels, call(): pl.pallas_call(kernel, out_shape=out, in_specs=[vmem] * len(args), out_sp...  7.22 us

profile of v6, /device:TPU:1, one launch (start us, length us, event | category | flops | bytes accessed | tf_op | source)
XLA Modules:
  0.0 117.8 jit_solution(5681498404213654660)
XLA Ops:
  0.0 0.0 copy-start.3
  0.0 0.7 copy-done.3
  0.7 0.1 spread.1
  0.8 23.1 %all_to_all.30.p_ref = bf16[16,25,128]{2,1,0:T(8,128)(2,1)S(1)} all-to-all(bf16[16,25,128]{2,1,0:T(8,128)(2,1)S(1)} %spread.1), channel_id=1, replica_groups={{305,307,309,311,313,315,317,319,289,291,293,295,297,299,301,303},{304,..., dimensions={0} | all-to-all | bytes 204800 | tf_op jit(solution)/shard_map/all_to_all | solution.py:52
  23.9 0.0 copy-start
  23.9 0.2 chunk.1
  24.1 0.0 copy-start.1
  24.1 0.0 copy-start.2
  24.2 19.0 %all_to_all.31.w_ref = bf16[16,400,128]{2,1,0:T(8,128)(2,1)S(1)} all-to-all(bf16[16,400,128]{2,1,0:T(8,128)(2,1)S(1)} %chunk.1), channel_id=1, replica_groups={{305,273,369,337,433,401,497,465,49,17,113,81,177,145,241,209},{304,272..., dimensions={0} | all-to-all | bytes 3276800 | tf_op jit(solution)/shard_map/all_to_all | solution.py:52
  43.1 0.0 copy-done
  43.1 0.0 copy-done.1
  43.1 0.0 copy-done.2
  43.1 5.2 %layer.1 = s16[16,408,128]{2,1,0:T(8,128)(2,1)S(1)} custom-call(bf16[464,5120]{1,0:T(8,128)(2,1)S(1)} %bitcast.5, bf16[16,400,128]{2,1,0:T(8,128)(2,1)S(1)} %all_to_all.31.w_ref, f32[6,1,464]{2,1,0:T(1,128)S(1)} %bitcast.6, s32[6,1,464]{2,1,0:T(1,128)S(1)} %bitcast.7), custom_call_target="tpu_custom_call" | custom-call | tf_op jit(solution)/shard_map/layer/pallas_call | solution.py:233
  48.3 18.0 %all_to_all.32.q_ref = s16[16,408,128]{2,1,0:T(8,128)(2,1)S(1)} all-to-all(s16[16,408,128]{2,1,0:T(8,128)(2,1)S(1)} %layer.1), channel_id=1, replica_groups={{305,273,369,337,433,401,497,465,49,17,113,81,177,145,241,209},{304,272..., dimensions={0} | all-to-all | bytes 3342336 | tf_op jit(solution)/shard_map/all_to_all | solution.py:52
  66.3 0.8 plane_sum.1
  67.1 15.8 %all_to_all.33.q_ref = s16[16,32,128]{2,1,0:T(8,128)(2,1)S(1)} all-to-all(s16[16,32,128]{2,1,0:T(8,128)(2,1)S(1)} %plane_sum.1), channel_id=1, replica_groups={{305,307,309,311,313,315,317,319,289,291,293,295,297,299,301,303},{304,..., dimensions={0} | all-to-all | bytes 262144 | tf_op jit(solution)/shard_map/all_to_all | solution.py:52
  83.0 0.2 line_sum.1
  83.1 21.1 %all_to_all.34.s_ref = f32[32,1,128]{2,1,0:T(1,128)S(1)} all-to-all(f32[32,1,128]{2,1,0:T(1,128)S(1)} %get-tuple-element.7), channel_id=1, replica_groups={{305,273,369,337,433,401,497,465,49,17,113,81,177,145,241,209,304,272,3..., dimensions={0} | all-to-all | bytes 32768 | tf_op jit(solution)/shard_map/all_to_all | solution.py:52
  104.2 12.8 %all_to_all.35.s_ref = f32[16,1,128]{2,1,0:T(1,128)S(1)} all-to-all(f32[16,1,128]{2,1,0:T(1,128)S(1)} %again.1), channel_id=1, replica_groups={{305,307,309,311,313,315,317,319,289,291,293,295,297,299,301,303},{304,..., dimensions={0} | all-to-all | bytes 16384 | tf_op jit(solution)/shard_map/all_to_all | solution.py:52
  117.1 0.8 clip.1
  (1 shorter events, 0.0 us)
Async XLA Ops:
  0.0 0.7 copy-start.3
  23.9 19.2 %copy-start = (bf16[1,464,5120]{2,1,0:T(8,128)(2,1)S(1)}, bf16[1,464,5120]{2,1,0:T(8,128)(2,1)}, u32[]{:S(2)}) copy-start(bf16[1,464,5120]{2,1,0:T(8,128)(2,1)} %param.4) | copy-start | bytes 14254084
  24.1 19.0 %copy-start.1 = (f32[1,464,6]{1,0,2:T(1,128)S(1)}, f32[1,464,6]{1,0,2:T(1,128)}, u32[]{:S(2)}) copy-start(f32[1,464,6]{1,0,2:T(1,128)} %param.5) | copy-start | bytes 33412
  24.1 19.0 %copy-start.2 = (s32[1,464,6]{1,0,2:T(1,128)S(1)}, s32[1,464,6]{1,0,2:T(1,128)}, u32[]{:S(2)}) copy-start(s32[1,464,6]{1,0,2:T(1,128)} %param.6) | copy-start | bytes 33412
